TPU v7x, 8 devices: a whole 2x2x1 slice. The times are simulated.
8 devices in a mesh: rep: 1 (over z), pool: 8 (over y, x, core).
Axes of the slice: x: 2, y: 2, z: 1, core: 2. Of those that a mesh axis runs over, the one named last changes fastest.
Arguments:
- kv_pool: bfloat16 [4, 256, 2, 64, 20, 128], P(None, ('rep', 'pool'))
- page_idx: int32 [8, 8, 4], P(None, ('rep', 'pool'))
- tok_hidden: bfloat16 [8, 128, 2560], P(('rep', 'pool'))
- attn_norm: bfloat16 [4, 2560], replicated
- w_query: bfloat16 [4, 2560, 2560], replicated
- w_key: bfloat16 [4, 2560, 2560], replicated
- w_value: bfloat16 [4, 2560, 2560], replicated
- w_out: bfloat16 [4, 2560, 2560], replicated
- mlp_norm: bfloat16 [4, 2560], replicated
- w_gate: bfloat16 [4, 2560, 6912], replicated
- w_up: bfloat16 [4, 2560, 6912], replicated
- w_down: bfloat16 [4, 6912, 2560], replicated
Outputs:
- output: bfloat16 [8, 128, 2560], P(('rep', 'pool'))
All inputs are finite; a program needn't handle non-finite values.
Results may differ from a plain program's by a relative error of at most 0.02.
Values are sent between devices in bfloat16 or wider.
A program may use at most 2.75 GiB of HBM per device.

v0:
```python
import math
import jax
import jax.numpy as jnp
from jax import lax
from jax.sharding import PartitionSpec as P

NORM_EPS = 1e-6
ROPE_BASE = 10000.0


def rms_norm(vals, gain):
    vals_f = vals.astype(jnp.float32)
    inv_rms = lax.rsqrt(jnp.mean(vals_f * vals_f, axis=-1, keepdims=True) + NORM_EPS)
    return (vals_f * inv_rms * gain.astype(jnp.float32)).astype(jnp.bfloat16)


def rope_tables(offset, tokens, head_dim):
    positions = (offset + jnp.arange(tokens)).astype(jnp.float32)
    exponent = jnp.arange(head_dim // 2).astype(jnp.float32) * (-2.0 / head_dim)
    inv_freq = jnp.power(ROPE_BASE, exponent)
    angles = positions[:, None] * inv_freq[None, :]
    return jnp.cos(angles)[:, None, :], jnp.sin(angles)[:, None, :]


def apply_rope(proj, cosine, sine):
    half = proj.shape[-1] // 2
    first = proj[..., :half]
    second = proj[..., half:]
    return jnp.concatenate([first * cosine - second * sine, second * cosine + first * sine], axis=-1)


def attend(query, pages_kv, key_new, val_new):
    tokens = query.shape[-3]
    scale = 1.0 / math.sqrt(query.shape[-1])
    key_pre = pages_kv[..., :, 0, :, :, :]
    val_pre = pages_kv[..., :, 1, :, :, :]
    score_pre = jnp.einsum('...thd,...pshd->...thps', query, key_pre, preferred_element_type=jnp.float32) * scale
    score_new = jnp.einsum('...thd,...uhd->...thu', query, key_new, preferred_element_type=jnp.float32) * scale
    causal = jnp.arange(tokens)[None, :] <= jnp.arange(tokens)[:, None]
    score_new = jnp.where(causal[:, None, :], score_new, -1e30)
    row_max = jnp.maximum(jnp.max(score_pre, axis=(-2, -1)), jnp.max(score_new, axis=-1))
    exp_pre = jnp.exp(score_pre - row_max[..., None, None])
    exp_new = jnp.exp(score_new - row_max[..., None])
    row_sum = jnp.sum(exp_pre, axis=(-2, -1)) + jnp.sum(exp_new, axis=-1)
    prob_pre = (exp_pre / row_sum[..., None, None]).astype(jnp.bfloat16)
    prob_new = (exp_new / row_sum[..., None]).astype(jnp.bfloat16)
    mixed = jnp.einsum('...thps,...pshd->...thd', prob_pre, val_pre, preferred_element_type=jnp.float32)
    mixed = mixed + jnp.einsum('...thu,...uhd->...thd', prob_new, val_new, preferred_element_type=jnp.float32)
    return mixed.astype(jnp.bfloat16)


def decoder_layer(hidden, pages_kv, cosine, sine, layer_weights):
    gain_attn, q_weight, k_weight, v_weight, o_weight, gain_mlp, gate_weight, up_weight, down_weight = layer_weights
    head_shape = hidden.shape[:-1] + pages_kv.shape[-2:]
    normed = rms_norm(hidden, gain_attn)
    query = apply_rope(jnp.dot(normed, q_weight, preferred_element_type=jnp.float32).reshape(head_shape), cosine, sine).astype(jnp.bfloat16)
    key_new = apply_rope(jnp.dot(normed, k_weight, preferred_element_type=jnp.float32).reshape(head_shape), cosine, sine).astype(jnp.bfloat16)
    val_new = jnp.dot(normed, v_weight, preferred_element_type=jnp.float32).astype(jnp.bfloat16).reshape(head_shape)
    mixed = attend(query, pages_kv, key_new, val_new)
    attn_out = mixed.reshape(hidden.shape[:-1] + (q_weight.shape[1],))
    hidden = (hidden.astype(jnp.float32) + jnp.dot(attn_out, o_weight, preferred_element_type=jnp.float32)).astype(jnp.bfloat16)
    normed_mlp = rms_norm(hidden, gain_mlp)
    gate = jnp.dot(normed_mlp, gate_weight, preferred_element_type=jnp.float32)
    upper = jnp.dot(normed_mlp, up_weight, preferred_element_type=jnp.float32)
    inner = (jax.nn.silu(gate) * upper).astype(jnp.bfloat16)
    return (hidden.astype(jnp.float32) + jnp.dot(inner, down_weight, preferred_element_type=jnp.float32)).astype(jnp.bfloat16)


def solution(mesh):
    group = mesh.shape['pool']

    def local_program(kv_local, idx_local, hid_local, attn_norm, w_query, w_key, w_value, w_out, mlp_norm, w_gate, w_up, w_down):
        prefix = group * idx_local.shape[2] * kv_local.shape[3]
        cosine, sine = rope_tables(prefix, hid_local.shape[1], kv_local.shape[-1])
        page_rows = idx_local[:, 0, :].reshape(-1)
        hidden = hid_local[0]
        for layer in range(kv_local.shape[0]):
            outgoing = jnp.take(kv_local[layer], page_rows, axis=0)
            incoming = lax.all_to_all(outgoing, 'pool', 0, 0, tiled=True)
            layer_weights = (attn_norm[layer], w_query[layer], w_key[layer], w_value[layer], w_out[layer], mlp_norm[layer], w_gate[layer], w_up[layer], w_down[layer])
            hidden = decoder_layer(hidden, incoming, cosine, sine, layer_weights)
        return hidden[None]

    data_specs = (P(None, ('rep', 'pool')), P(None, ('rep', 'pool'), None), P(('rep', 'pool')))
    return jax.shard_map(local_program, mesh=mesh, in_specs=data_specs + (P(),) * 9, out_specs=P(('rep', 'pool')), check_vma=False)
```

profile of v0, /device:TPU:0, one launch (start us, length us, event | category | flops | bytes accessed | tf_op | source)
XLA Modules:
  0.0 1225.1 jit_solution(17128436075583863533)
XLA Ops:
  0.9 67.3 %slice_bitcast_fusion = (bf16[32,2,64,20,128]{4,2,3,1,0:T(8,128)(2,1)}, bf16[32,2,64,20,128]{4,2,3,1,0:T(8,128)(2,1)}, bf16[32,2,64,20,128]{4,2,3,1,0:T(8,128)(2,1)}, bf16[32,2,64,20,128]{4,2,3,1,0:T(8,128)(2,1)}) fusion(bf16[4,32,2,64,20,128]{5,3,4,2,1,0:T(8,128)(2,1)} %param.14), kind=kLoop, calls=%fused_computation.53 | loop fusion | bytes 167772160 | tf_op jit(solution)/shard_map/squeeze | solution.py:78
  68.2 15.7 %gather_fusion.3 = bf16[32,2,64,20,128]{4,2,3,1,0:T(8,128)(2,1)} fusion(bf16[32,2,64,20,128]{4,2,3,1,0:T(8,128)(2,1)} %get-tuple-element.14, s32[1024]{0:T(1024)S(1)} %pad_clamp_fusion), kind=kCustom, calls=%fused_computation.3.clone | custom fusion | bytes 41943168 | tf_op jit(solution)/shard_map/jit(_take)/gather | solution.py:78
  83.9 15.7 %gather_fusion.1 = bf16[32,2,64,20,128]{4,2,3,1,0:T(8,128)(2,1)} fusion(bf16[32,2,64,20,128]{4,2,3,1,0:T(8,128)(2,1)} %get-tuple-element.15, s32[1024]{0:T(1024)S(1)} %pad_clamp_fusion), kind=kCustom, calls=%fused_computation.1.clone | custom fusion | bytes 41943168 | tf_op jit(solution)/shard_map/jit(_take)/gather | solution.py:78
  99.6 15.8 %gather_fusion.2 = bf16[32,2,64,20,128]{4,2,3,1,0:T(8,128)(2,1)} fusion(bf16[32,2,64,20,128]{4,2,3,1,0:T(8,128)(2,1)} %get-tuple-element.17, s32[1024]{0:T(1024)S(1)} %pad_clamp_fusion), kind=kCustom, calls=%fused_computation.2.clone | custom fusion | bytes 41943168 | tf_op jit(solution)/shard_map/jit(_take)/gather | solution.py:78
  115.3 15.7 %gather_fusion = bf16[32,2,64,20,128]{4,2,3,1,0:T(8,128)(2,1)} fusion(bf16[32,2,64,20,128]{4,2,3,1,0:T(8,128)(2,1)} %get-tuple-element.16, s32[1024]{0:T(1024)S(1)} %pad_clamp_fusion), kind=kCustom, calls=%fused_computation.clone | custom fusion | bytes 41943168 | tf_op jit(solution)/shard_map/jit(_take)/gather | solution.py:78
  131.0 53.1 %broadcast_select_fusion = (bf16[32,2,64,20,128]{4,2,3,1,0:T(8,128)(2,1)}, bf16[32,2,64,20,128]{4,2,3,1,0:T(8,128)(2,1)}, bf16[32,2,64,20,128]{4,2,3,1,0:T(8,128)(2,1)}, bf16[32,2,64,20,128]{4,2,3,1,0:T(8,128)(2,1)}) fusion(bf16[32,2,64,20,128]{4,2,3,1,0:T(8,128)(2,1)} %gather_fusion.3, pred[32]{0:T(512)(128)(4,1)S(1)} %compare_and_fusion, ...), kind=kLoop, calls=%fused_computation.60 | loop fusion | flops 41943040 | bytes 167772192 | tf_op jit(solution)/shard_map/jit(_take)/select_n | solution.py:78
  189.1 35.7 %slice_bitcast_fusion.4 = (bf16[2560,2560]{0,1:T(8,128)(2,1)}, bf16[2560,2560]{0,1:T(8,128)(2,1)}, bf16[2560,2560]{0,1:T(8,128)(2,1)}, bf16[2560,2560]{0,1:T(8,128)(2,1)}) fusion(bf16[4,2560,2560]{2,1,0:T(8,128)(2,1)} %param.19), kind=kLoop, calls=%fused_computation.86 | loop fusion | bytes 104857600 | tf_op jit(solution)/shard_map/dot_general | solution.py:57
  224.8 17.6 %copy.80 = bf16[2560,2560]{1,0:T(8,128)(2,1)} copy(bf16[2560,2560]{0,1:T(8,128)(2,1)} %get-tuple-element.20) | data formatting | bytes 26214400 | tf_op jit(solution)/shard_map/dot_general | solution.py:57
  242.4 35.8 %slice_bitcast_fusion.5 = (bf16[2560,2560]{0,1:T(8,128)(2,1)}, bf16[2560,2560]{0,1:T(8,128)(2,1)}, bf16[2560,2560]{0,1:T(8,128)(2,1)}, bf16[2560,2560]{0,1:T(8,128)(2,1)}) fusion(bf16[4,2560,2560]{2,1,0:T(8,128)(2,1)} %param.18), kind=kLoop, calls=%fused_computation.87 | loop fusion | bytes 104857600 | tf_op jit(solution)/shard_map/dot_general | solution.py:56
  278.2 17.7 %copy.78 = bf16[2560,2560]{1,0:T(8,128)(2,1)} copy(bf16[2560,2560]{0,1:T(8,128)(2,1)} %get-tuple-element.24) | data formatting | bytes 26214400 | tf_op jit(solution)/shard_map/dot_general | solution.py:56
  304.6 17.6 %copy.89 = bf16[2560,2560]{1,0:T(8,128)(2,1)} copy(bf16[2560,2560]{0,1:T(8,128)(2,1)} %get-tuple-element.19) | data formatting | bytes 26214400 | tf_op jit(solution)/shard_map/dot_general | solution.py:57
  322.2 17.6 %copy.87 = bf16[2560,2560]{1,0:T(8,128)(2,1)} copy(bf16[2560,2560]{0,1:T(8,128)(2,1)} %get-tuple-element.23) | data formatting | bytes 26214400 | tf_op jit(solution)/shard_map/dot_general | solution.py:56
  339.8 17.6 %copy.98 = bf16[2560,2560]{1,0:T(8,128)(2,1)} copy(bf16[2560,2560]{0,1:T(8,128)(2,1)} %get-tuple-element.21) | data formatting | bytes 26214400 | tf_op jit(solution)/shard_map/dot_general | solution.py:57
  357.3 17.6 %copy.96 = bf16[2560,2560]{1,0:T(8,128)(2,1)} copy(bf16[2560,2560]{0,1:T(8,128)(2,1)} %get-tuple-element.25) | data formatting | bytes 26214400 | tf_op jit(solution)/shard_map/dot_general | solution.py:56
  375.0 17.6 %copy.107 = bf16[2560,2560]{1,0:T(8,128)(2,1)} copy(bf16[2560,2560]{0,1:T(8,128)(2,1)} %get-tuple-element.18) | data formatting | bytes 26214400 | tf_op jit(solution)/shard_map/dot_general | solution.py:57
  392.6 17.6 %copy.105 = bf16[2560,2560]{1,0:T(8,128)(2,1)} copy(bf16[2560,2560]{0,1:T(8,128)(2,1)} %get-tuple-element.22) | data formatting | bytes 26214400 | tf_op jit(solution)/shard_map/dot_general | solution.py:56
  430.6 15.0 %fusion.325 = (bf16[32,1,64,20,128]{4,2,3,1,0:T(8,128)(2,1)}, bf16[32,1,64,20,128]{4,2,3,1,0:T(8,128)(2,1)S(1)}) fusion(bf16[32,2,64,20,128]{4,2,3,1,0:T(8,128)(2,1)} %all-to-all-done), kind=kLoop, calls=%fused_computation.348 | loop fusion | bytes 41943040 | tf_op jit(solution)/shard_map/slice | solution.py:36
  484.1 15.5 %fusion.22 = f32[128,6912]{1,0:T(8,128)} fusion(bf16[4,2560,6912]{2,1,0:T(8,128)(2,1)} %param.23, f32[128,2560]{1,0:T(8,128)S(1)} %get-tuple-element.69, f32[2560]{0:T(1024)S(1)} %get-tuple-element.8, f32[128]{0:T(128)S(1)} %add_rsqrt_fusion.6), kind=kOutput, calls=%fused_computation.26 | convolution fusion | flops 4530831360 | bytes 40249856 | tf_op jit(solution)/shard_map/dot_general | solution.py:63
  499.7 30.9 %multiply_reduce_fusion.5 = (f32[128]{0:T(128)S(1)}, f32[128,2560]{1,0:T(8,128)S(1)}) fusion(f32[128,2560]{1,0:T(8,128)} %copy-done.26, bf16[4,6912,2560]{2,1,0:T(8,128)(2,1)} %param.25, bf16[4,2560,6912]{2,1,0:T(8,128)(2,1)} %param.24, f32[128,6912]{1,0:T(8,128)} %fusion.22, f32[2560]{0:T(1024)S(1)} %get-tuple-element.8, f32[128]{0:T(128)S(1)} %add_rsqrt_fusion.6), kind=kOutput, calls=%fused_computation.219 | convolution fusion | flops 9067626496 | bytes 78261248 | tf_op jit(solution)/shard_map/dot_general | solution.py:66
  551.4 109.1 %all-to-all-done.1 = bf16[32,2,64,20,128]{4,2,3,1,0:T(8,128)(2,1)} async-done(((bf16[32,2,64,20,128]{4,2,3,1,0:T(8,128)(2,1)}), bf16[32,2,64,20,128]{4,2,3,1,0:T(8,128)(2,1)}, u32[]{:S(2)}, u32[]{:S(2)}) %all-to-all-start.1) | async-done | bytes 20971552 | tf_op jit(solution)/shard_map/all_to_all | solution.py:79
  665.5 14.9 %fusion.324 = (bf16[32,1,64,20,128]{4,2,3,1,0:T(8,128)(2,1)}, bf16[32,1,64,20,128]{4,2,3,1,0:T(8,128)(2,1)S(1)}) fusion(bf16[32,2,64,20,128]{4,2,3,1,0:T(8,128)(2,1)} %all-to-all-done.1), kind=kLoop, calls=%fused_computation.347 | loop fusion | bytes 41943040 | tf_op jit(solution)/shard_map/slice | solution.py:36
  718.3 15.6 %fusion.16 = f32[128,6912]{1,0:T(8,128)} fusion(bf16[4,2560,6912]{2,1,0:T(8,128)(2,1)} %param.23, f32[128,2560]{1,0:T(8,128)S(1)} %get-tuple-element.77, f32[2560]{0:T(1024)S(1)} %copy-done.25, f32[128]{0:T(128)S(1)} %add_rsqrt_fusion.4), kind=kOutput, calls=%fused_computation.20 | convolution fusion | flops 4530831360 | bytes 40249856 | tf_op jit(solution)/shard_map/dot_general | solution.py:63
  733.9 25.9 %multiply_reduce_fusion.3 = (f32[128]{0:T(128)S(1)}, f32[128,2560]{1,0:T(8,128)S(1)}) fusion(f32[128,2560]{1,0:T(8,128)S(1)} %get-tuple-element.77, bf16[4,6912,2560]{2,1,0:T(8,128)(2,1)} %param.25, bf16[4,2560,6912]{2,1,0:T(8,128)(2,1)} %param.24, f32[128,6912]{1,0:T(8,128)} %fusion.16, f32[2560]{0:T(1024)S(1)} %copy-done.25, f32[128]{0:T(128)S(1)} %add_rsqrt_fusion.4), kind=kOutput, calls=%fused_computation.213 | convolution fusion | flops 9067626496 | bytes 78263296 | tf_op jit(solution)/shard_map/dot_general | solution.py:66
  780.7 113.7 %all-to-all-done.2 = bf16[32,2,64,20,128]{4,2,3,1,0:T(8,128)(2,1)} async-done(((bf16[32,2,64,20,128]{4,2,3,1,0:T(8,128)(2,1)}), bf16[32,2,64,20,128]{4,2,3,1,0:T(8,128)(2,1)}, u32[]{:S(2)}, u32[]{:S(2)}) %all-to-all-start.2) | async-done | bytes 20971552 | tf_op jit(solution)/shard_map/all_to_all | solution.py:79
  899.7 14.9 %fusion.323 = (bf16[32,1,64,20,128]{4,2,3,1,0:T(8,128)(2,1)}, bf16[32,1,64,20,128]{4,2,3,1,0:T(8,128)(2,1)S(1)}) fusion(bf16[32,2,64,20,128]{4,2,3,1,0:T(8,128)(2,1)} %all-to-all-done.2), kind=kLoop, calls=%fused_computation.346 | loop fusion | bytes 41943040 | tf_op jit(solution)/shard_map/slice | solution.py:36
  952.4 15.6 %fusion.10 = f32[128,6912]{1,0:T(8,128)} fusion(bf16[4,2560,6912]{2,1,0:T(8,128)(2,1)} %param.23, f32[128,2560]{1,0:T(8,128)S(1)} %get-tuple-element.85, f32[2560]{0:T(1024)S(1)} %copy-done.24, f32[128]{0:T(128)S(1)} %add_rsqrt_fusion.2), kind=kOutput, calls=%fused_computation.14 | convolution fusion | flops 4530831360 | bytes 40249856 | tf_op jit(solution)/shard_map/dot_general | solution.py:63
  968.0 26.0 %multiply_reduce_fusion.1 = (f32[128]{0:T(128)S(1)}, f32[128,2560]{1,0:T(8,128)S(1)}) fusion(f32[128,2560]{1,0:T(8,128)S(1)} %get-tuple-element.85, bf16[4,6912,2560]{2,1,0:T(8,128)(2,1)} %param.25, bf16[4,2560,6912]{2,1,0:T(8,128)(2,1)} %param.24, f32[128,6912]{1,0:T(8,128)} %fusion.10, f32[2560]{0:T(1024)S(1)} %copy-done.24, f32[128]{0:T(128)S(1)} %add_rsqrt_fusion.2), kind=kOutput, calls=%fused_computation.207 | convolution fusion | flops 9067626496 | bytes 78263296 | tf_op jit(solution)/shard_map/dot_general | solution.py:66
  1016.2 112.4 %all-to-all-done.3 = bf16[32,2,64,20,128]{4,2,3,1,0:T(8,128)(2,1)} async-done(((bf16[32,2,64,20,128]{4,2,3,1,0:T(8,128)(2,1)}), bf16[32,2,64,20,128]{4,2,3,1,0:T(8,128)(2,1)}, u32[]{:S(2)}, u32[]{:S(2)}) %all-to-all-start.3) | async-done | bytes 20971552 | tf_op jit(solution)/shard_map/all_to_all | solution.py:79
  1128.6 14.9 %fusion.322 = (bf16[32,1,64,20,128]{4,2,3,1,0:T(8,128)(2,1)}, bf16[32,1,64,20,128]{4,2,3,1,0:T(8,128)(2,1)S(1)}) fusion(bf16[32,2,64,20,128]{4,2,3,1,0:T(8,128)(2,1)} %all-to-all-done.3), kind=kLoop, calls=%fused_computation.345 | loop fusion | bytes 41943040 | tf_op jit(solution)/shard_map/slice | solution.py:36
  1162.9 13.5 %fusion.226 = f32[20,128,128]{2,1,0:T(8,128)S(1)} fusion(f32[20,32,64,128]{3,2,1,0:T(8,128)} %get-tuple-element.89, f32[128,20]{0,1:T(8,128)S(1)} %add.295, f32[128,20]{0,1:T(8,128)S(1)} %max.47, bf16[32,1,64,20,128]{4,2,3,1,0:T(8,128)(2,1)} %get-tuple-element.26), kind=kOutput, calls=%fused_computation.194 | convolution fusion | flops 1363148800 | bytes 32788480 | tf_op jit(solution)/shard_map/...thps,...pshd->...thd/dot_general | solution.py:47
  1182.8 15.6 %fusion.4 = f32[128,6912]{1,0:T(8,128)} fusion(bf16[4,2560,6912]{2,1,0:T(8,128)(2,1)} %param.23, f32[128,2560]{1,0:T(8,128)S(1)} %get-tuple-element.93, f32[2560]{0:T(1024)S(1)} %copy-done.23, f32[128]{0:T(128)S(1)} %add_rsqrt_fusion), kind=kOutput, calls=%fused_computation.8 | convolution fusion | flops 4530831360 | bytes 40249856 | tf_op jit(solution)/shard_map/dot_general | solution.py:63
  1198.4 26.5 %fusion.205 = bf16[1,128,2560]{2,1,0:T(8,128)(2,1)} fusion(f32[128,2560]{1,0:T(8,128)S(1)} %get-tuple-element.93, bf16[4,6912,2560]{2,1,0:T(8,128)(2,1)} %param.25, bf16[4,2560,6912]{2,1,0:T(8,128)(2,1)} %param.24, f32[128,6912]{1,0:T(8,128)} %fusion.4, f32[2560]{0:T(1024)S(1)} %copy-done.23, f32[128]{0:T(128)S(1)} %add_rsqrt_fusion), kind=kOutput, calls=%fused_computation.167 | convolution fusion | flops 9066643456 | bytes 77607424 | tf_op jit(solution)/shard_map/dot_general | solution.py:66
  (137 shorter events, 248.4 us)
Async XLA Ops:
  184.1 241.4 %all-to-all-start = ((bf16[32,2,64,20,128]{4,2,3,1,0:T(8,128)(2,1)}), bf16[32,2,64,20,128]{4,2,3,1,0:T(8,128)(2,1)}, u32[]{:S(2)}, u32[]{:S(2)}) async-start(bf16[32,2,64,20,128]{4,2,3,1,0:T(8,128)(2,1)} %get-tuple-element.63), calls=%async_computation | async-start | bytes 41943040 | tf_op jit(solution)/shard_map/all_to_all | solution.py:79
  278.2 17.7 %copy-start.14 = (bf16[4,2560]{1,0:T(4,128)(2,1)S(1)}, bf16[4,2560]{1,0:T(4,128)(2,1)}, u32[]{:S(2)}) copy-start(bf16[4,2560]{1,0:T(4,128)(2,1)} %param.17) | copy-start | bytes 61444
  278.2 18.4 %copy-start = (bf16[1,128,2560]{2,1,0:T(8,128)(2,1)S(1)}, bf16[1,128,2560]{2,1,0:T(8,128)(2,1)}, u32[]{:S(2)}) copy-start(bf16[1,128,2560]{2,1,0:T(8,128)(2,1)} %param.16) | copy-start | bytes 1966084
  392.6 17.6 %copy-start.15 = (bf16[4,2560]{1,0:T(4,128)(2,1)S(1)}, bf16[4,2560]{1,0:T(4,128)(2,1)}, u32[]{:S(2)}) copy-start(bf16[4,2560]{1,0:T(4,128)(2,1)} %param.22) | copy-start | bytes 61444
  410.2 14.9 %copy-start.19 = (pred[128,128]{0,1:T(8,128)(4,1)}, pred[128,128]{0,1:T(8,128)(4,1)S(1)}, u32[]{:S(2)}) copy-start(pred[128,128]{0,1:T(8,128)(4,1)S(1)} %iota_compare_fusion) | copy-start | bytes 49156
  411.1 13.6 %copy-start.1 = (f32[128,64]{0,1:T(8,128)}, f32[128,64]{0,1:T(8,128)S(1)}, u32[]{:S(2)}) copy-start(f32[128,64]{0,1:T(8,128)S(1)} %get-tuple-element.58) | copy-start | bytes 98308
  411.1 13.6 %copy-start.5 = (f32[128,64]{0,1:T(8,128)}, f32[128,64]{0,1:T(8,128)S(1)}, u32[]{:S(2)}) copy-start(f32[128,64]{0,1:T(8,128)S(1)} %get-tuple-element.59) | copy-start | bytes 98308
  425.5 234.9 %all-to-all-start.1 = ((bf16[32,2,64,20,128]{4,2,3,1,0:T(8,128)(2,1)}), bf16[32,2,64,20,128]{4,2,3,1,0:T(8,128)(2,1)}, u32[]{:S(2)}, u32[]{:S(2)}) async-start(bf16[32,2,64,20,128]{4,2,3,1,0:T(8,128)(2,1)} %get-tuple-element.61), calls=%async_computation.1 | async-start | bytes 41943040 | tf_op jit(solution)/shard_map/all_to_all | solution.py:79
  463.3 13.4 %copy-start.9 = (bf16[128,2560]{0,1:T(8,128)(2,1)S(1)}, bf16[128,2560]{0,1:T(8,128)(2,1)}, u32[]{:S(2)}) copy-start(bf16[128,2560]{0,1:T(8,128)(2,1)} %copy.83) | copy-start | bytes 1966084
  483.1 1.1 copy-start.26
  499.7 30.9 %copy-start.18 = (f32[2560]{0:T(1024)S(1)}, f32[2560]{0:T(1024)}, u32[]{:S(2)}) copy-start(f32[2560]{0:T(1024)} %get-tuple-element.11) | copy-start | bytes 30724
  544.3 6.7 copy-start.2
  544.3 6.7 copy-start.6
  660.5 234.0 %all-to-all-start.2 = ((bf16[32,2,64,20,128]{4,2,3,1,0:T(8,128)(2,1)}), bf16[32,2,64,20,128]{4,2,3,1,0:T(8,128)(2,1)}, u32[]{:S(2)}, u32[]{:S(2)}) async-start(bf16[32,2,64,20,128]{4,2,3,1,0:T(8,128)(2,1)} %get-tuple-element.62), calls=%async_computation.2 | async-start | bytes 41943040 | tf_op jit(solution)/shard_map/all_to_all | solution.py:79
  680.4 8.5 copy-start.20
  712.3 6.0 copy-start.25
  733.9 26.0 %copy-start.17 = (f32[2560]{0:T(1024)S(1)}, f32[2560]{0:T(1024)}, u32[]{:S(2)}) copy-start(f32[2560]{0:T(1024)} %get-tuple-element.13) | copy-start | bytes 30724
  773.6 6.7 copy-start.3
  773.6 6.7 copy-start.7
  894.4 234.2 %all-to-all-start.3 = ((bf16[32,2,64,20,128]{4,2,3,1,0:T(8,128)(2,1)}), bf16[32,2,64,20,128]{4,2,3,1,0:T(8,128)(2,1)}, u32[]{:S(2)}, u32[]{:S(2)}) async-start(bf16[32,2,64,20,128]{4,2,3,1,0:T(8,128)(2,1)} %get-tuple-element.60), calls=%async_computation.3 | async-start | bytes 41943040 | tf_op jit(solution)/shard_map/all_to_all | solution.py:79
  914.6 8.5 copy-start.21
  946.4 6.0 copy-start.24
  968.0 26.0 %copy-start.16 = (f32[2560]{0:T(1024)S(1)}, f32[2560]{0:T(1024)}, u32[]{:S(2)}) copy-start(f32[2560]{0:T(1024)} %get-tuple-element.10) | copy-start | bytes 30724
  1000.9 6.7 copy-start.4
  1000.9 6.7 copy-start.8
  1143.5 8.5 copy-start.12
  1143.5 8.5 copy-start.13
  1143.5 8.5 copy-start.22
  1152.5 9.3 copy-start.10
  1162.9 13.5 %copy-start.11 = (bf16[128,2560]{0,1:T(8,128)(2,1)S(1)}, bf16[128,2560]{0,1:T(8,128)(2,1)}, u32[]{:S(2)}) copy-start(bf16[128,2560]{0,1:T(8,128)(2,1)} %copy.110) | copy-start | bytes 1966084
  1176.8 6.0 copy-start.23
where the time goes:
time: 1230 us
  local copies, waits for them, and re-layouts  407 us (33%)
  matrix products  367 us (30%)
  waiting for transfers between devices  335 us (27%)
  other arithmetic  94.7 us (8%)
  starting transfers between devices  20.3 us (2%)
    all_to_all x4, waiting for transfers between devices, local_program(): incoming = lax.all_to_all(outgoing, 'pool', 0, 0, tiled=True)  335 us
    dot_general x4, matrix products, decoder_layer(): jnp.dot(inner, down_weight, preferred_element_type=jnp.float32)  109 us
    dot_general x5, local copies, waits for them, and re-layouts, decoder_layer(): jnp.dot(normed, q_weight, preferred_element_type=jnp.float32)  106 us
    dot_general x5, local copies, waits for them, and re-layouts, decoder_layer(): jnp.dot(normed, k_weight, preferred_element_type=jnp.float32)  106 us
    squeeze x1, local copies, waits for them, and re-layouts, local_program(): outgoing = jnp.take(kv_local[layer], page_rows, axis=0)  67.3 us
    gather x4, local copies, waits for them, and re-layouts, local_program(): outgoing = jnp.take(kv_local[layer], page_rows, axis=0)  62.8 us
    dot_general x4, matrix products, decoder_layer(): gate = jnp.dot(normed_mlp, gate_weight, preferred_element_type=jnp.float32)  62.4 us
    slice x4, local copies, waits for them, and re-layouts, attend(): val_pre = pages_kv[..., :, 1, :, :, :]  59.8 us
  transfers between devices with their start and end apart: 4, of which 3 were waited for; matrix products, arithmetic and copies ran while one was open for 48% of the time, Pallas kernels for 0%

commit v1 on v0

v1 whole, which is shorter than its diff:
```python
import functools
import math
import jax
import jax.numpy as jnp
from jax import lax
from jax.experimental import pallas as pl
from jax.experimental.pallas import tpu as pltpu
from jax.sharding import PartitionSpec as P

NORM_EPS = 1e-6
ROPE_BASE = 10000.0
GROUP_HEADS = 2
Q_AHEAD = 3
MESH = pl.DeviceIdType.MESH


def rope_tables(offset, tokens, head_dim):
    positions = (offset + jnp.arange(tokens)).astype(jnp.float32)
    exponent = jnp.arange(head_dim // 2).astype(jnp.float32) * (-2.0 / head_dim)
    inv_freq = jnp.power(ROPE_BASE, exponent)
    angles = positions[:, None] * inv_freq[None, :]
    cosine, sine = jnp.cos(angles), jnp.sin(angles)
    return jnp.concatenate([cosine, cosine], axis=-1), jnp.concatenate([-sine, sine], axis=-1)


def rms_rows(vals, gain):
    inv_rms = lax.rsqrt(jnp.mean(vals * vals, axis=-1, keepdims=True) + NORM_EPS)
    return (vals * inv_rms * gain).astype(jnp.bfloat16)


def qkv_kernel(layer, head_dim, x_ref, gain_ref, cos_ref, sin_ref, wq_ref, wk_ref, wv_ref, q_ref, k_ref, v_ref, h_ref):
    @pl.when(pl.program_id(0) == 0)
    def _():
        h_ref[...] = rms_rows(x_ref[...].astype(jnp.float32), gain_ref[layer : layer + 1, :].astype(jnp.float32))

    normed = h_ref[...]
    cosine, sine = cos_ref[...], sin_ref[...]
    for w_ref, o_ref in ((wq_ref, q_ref), (wk_ref, k_ref)):
        proj = jnp.dot(normed, w_ref[...], preferred_element_type=jnp.float32)
        for h in range(GROUP_HEADS):
            part = proj[:, h * head_dim : (h + 1) * head_dim]
            turned = part * cosine + pltpu.roll(part, head_dim // 2, 1) * sine
            o_ref[:, h * head_dim : (h + 1) * head_dim] = turned.astype(jnp.bfloat16)
    v_ref[...] = jnp.dot(normed, wv_ref[...], preferred_element_type=jnp.float32).astype(jnp.bfloat16)


def project_qkv(layer, hidden, gain, cosine, sine, wq, wk, wv, head_dim):
    tokens, width = hidden.shape
    cols = GROUP_HEADS * head_dim
    steps = wq.shape[2] // cols
    whole = lambda a: pl.BlockSpec(a.shape, lambda j: (0,) * a.ndim)
    wspec = pl.BlockSpec((None, width, cols), lambda j: (layer, 0, j))
    ospec = pl.BlockSpec((None, tokens, cols), lambda j: (j, 0, 0))
    oshape = jax.ShapeDtypeStruct((steps, tokens, cols), jnp.bfloat16)
    return pl.pallas_call(
        functools.partial(qkv_kernel, layer, head_dim),
        grid=(steps,),
        in_specs=[whole(hidden), whole(gain), whole(cosine), whole(sine), wspec, wspec, wspec],
        out_specs=[ospec] * 3,
        out_shape=[oshape] * 3,
        scratch_shapes=[pltpu.VMEM((tokens, width), jnp.bfloat16)],
        compiler_params=pltpu.CompilerParams(dimension_semantics=("arbitrary",)),
        name="qkv",
    )(hidden, gain, cosine, sine, wq, wk, wv)


def mlp_kernel(layer, o_steps, o_cols, x_ref, a_ref, gain_ref, wo_ref, wg_ref, wu_ref, wd_ref, out_ref, x1_ref, h_ref, acc_ref):
    step = pl.program_id(0)

    @pl.when(step < o_steps)
    def _():
        cols = pl.ds(pl.multiple_of(step * o_cols, o_cols), o_cols)
        proj = jnp.dot(a_ref[...], wo_ref[...], preferred_element_type=jnp.float32)
        x1_ref[:, cols] = (x_ref[:, cols].astype(jnp.float32) + proj).astype(jnp.bfloat16)

    @pl.when(step == o_steps)
    def _():
        h_ref[...] = rms_rows(x1_ref[...].astype(jnp.float32), gain_ref[layer : layer + 1, :].astype(jnp.float32))
        acc_ref[...] = jnp.zeros_like(acc_ref)

    @pl.when(step >= o_steps)
    def _():
        normed = h_ref[...]
        gate = jnp.dot(normed, wg_ref[...], preferred_element_type=jnp.float32)
        upper = jnp.dot(normed, wu_ref[...], preferred_element_type=jnp.float32)
        inner = (jax.nn.silu(gate) * upper).astype(jnp.bfloat16)
        acc_ref[...] += jnp.dot(inner, wd_ref[...], preferred_element_type=jnp.float32)

    @pl.when(step == pl.num_programs(0) - 1)
    def _():
        out_ref[...] = (x1_ref[...].astype(jnp.float32) + acc_ref[...]).astype(jnp.bfloat16)


def out_and_mlp(layer, hidden, attn, gain, wo, wg, wu, wd):
    tokens, width = hidden.shape
    o_cols, f_cols = 256, 384
    o_steps, f_steps = width // o_cols, wg.shape[2] // f_cols
    whole = lambda a: pl.BlockSpec(a.shape, lambda j: (0,) * a.ndim)
    ff = lambda j: jnp.maximum(j - o_steps, 0)
    return pl.pallas_call(
        functools.partial(mlp_kernel, layer, o_steps, o_cols),
        grid=(o_steps + f_steps,),
        in_specs=[
            whole(hidden),
            whole(attn),
            whole(gain),
            pl.BlockSpec((None, wo.shape[1], o_cols), lambda j: (layer, 0, jnp.minimum(j, o_steps - 1))),
            pl.BlockSpec((None, width, f_cols), lambda j: (layer, 0, ff(j))),
            pl.BlockSpec((None, width, f_cols), lambda j: (layer, 0, ff(j))),
            pl.BlockSpec((None, f_cols, width), lambda j: (layer, ff(j), 0)),
        ],
        out_specs=whole(hidden),
        out_shape=jax.ShapeDtypeStruct(hidden.shape, jnp.bfloat16),
        scratch_shapes=[
            pltpu.VMEM((tokens, width), jnp.bfloat16),
            pltpu.VMEM((tokens, width), jnp.bfloat16),
            pltpu.VMEM((tokens, width), jnp.float32),
        ],
        compiler_params=pltpu.CompilerParams(dimension_semantics=("arbitrary",)),
        name="out_mlp",
    )(hidden, attn, gain, wo, wg, wu, wd)


def stat_rows(maxes, sums):
    rows = [r for pair in zip(maxes, sums) for r in pair]
    index = lax.broadcasted_iota(jnp.int32, (8, rows[0].shape[-1]), 0)
    block = jnp.zeros((8, rows[0].shape[-1]), jnp.float32)
    for n, row in enumerate(rows):
        block = jnp.where(index == n, row, block)
    return block


def merge_into(dst, src, dim):
    base = GROUP_HEADS * dim
    one, two = dst[base : base + 8, :], src[base : base + 8, :]
    maxes, sums = [], []
    for h in range(GROUP_HEADS):
        m1, m2 = one[2 * h : 2 * h + 1], two[2 * h : 2 * h + 1]
        top = jnp.maximum(m1, m2)
        a1, a2 = jnp.exp2(m1 - top), jnp.exp2(m2 - top)
        rows = slice(h * dim, (h + 1) * dim)
        dst[rows, :] = dst[rows, :] * a1 + src[rows, :] * a2
        maxes.append(top)
        sums.append(one[2 * h + 1 : 2 * h + 2] * a1 + two[2 * h + 1 : 2 * h + 2] * a2)
    dst[base : base + 8, :] = stat_rows(maxes, sums)


def partial_attention(dst, query, key_of, val_of, scale, dim, mask=None):
    maxes, sums = [], []
    for h in range(GROUP_HEADS):
        score = lax.dot_general(
            key_of(h), query[:, h * dim : (h + 1) * dim], (((1,), (1,)), ((), ())), preferred_element_type=jnp.float32
        )
        score = score * scale
        if mask is not None:
            score = jnp.where(mask, score, -1e30)
        top = jnp.max(score, axis=0, keepdims=True)
        expo = jnp.exp2(score - top)
        sums.append(jnp.sum(expo, axis=0, keepdims=True))
        maxes.append(top)
        dst[h * dim : (h + 1) * dim, :] = lax.dot_general(
            val_of(h), expo.astype(jnp.bfloat16), (((0,), (0,)), ((), ())), preferred_element_type=jnp.float32
        )
    dst[GROUP_HEADS * dim : GROUP_HEADS * dim + 8, :] = stat_rows(maxes, sums)


def attn_kernel(
    layer, groups, dim,
    idx_ref, q_ref, kn_ref, vn_ref, kv_ref, a_ref,
    kvb, kvo, qall, part, prx, rel, fin,
    kv_sem, qs_sem, qr_sem, ps_sem, pr_sem, ds_sem, dr_sem, fs_sem, fr_sem,
):
    me = lax.axis_index("pool")
    rep = lax.axis_index("rep")
    core = me % 2
    xpos = (me // 2) % 2
    ypos = me // 4
    scale = math.log2(math.e) / math.sqrt(dim)
    tokens = q_ref.shape[1]
    page_len = kvb.shape[3]

    def at(flip_y, flip_x, flip_core):
        return (((ypos + flip_y) % 2) * 2 + (xpos + flip_x) % 2) * 2 + (core + flip_core) % 2

    mate, xdev, ydev = (rep, at(0, 0, 1)), (rep, at(0, 1, 0)), (rep, at(1, 0, 0))

    def remote(src, dst, ssem, rsem, dev):
        return pltpu.make_async_remote_copy(src, dst, ssem, rsem, device_id=dev, device_id_type=MESH)

    def q_own(n, g):
        slot, dev = ((1, xdev), (2, ydev), (4, mate))[n]
        return remote(q_ref.at[g], qall.at[slot, g], qs_sem.at[n, g], qr_sem.at[slot, g], dev)

    def q_mate(slot, g):
        return remote(qall.at[slot, g], qall.at[slot + 4, g], qs_sem.at[2 + slot, g], qr_sem.at[slot + 4, g], mate)

    def q_relay(via_x, g):
        slot, dev = (1, ydev) if via_x else (2, xdev)
        return remote(qall.at[slot, g], qall.at[3, g], qs_sem.at[6, g], qr_sem.at[3, g], dev)

    def to_mate(n, g):
        return remote(part.at[4 + n, g], prx.at[n, g], ps_sem.at[n, g], pr_sem.at[n, g], mate)

    def diag_send(via_x, g):
        return remote(part.at[3, g], rel.at[g], ds_sem.at[g], dr_sem.at[g], xdev if via_x else ydev)

    def home_send(n, g):
        return remote(part.at[1 + n, g], fin.at[n, g], fs_sem.at[n, g], fr_sem.at[n, g], xdev if n == 0 else ydev)

    def kv_copy(g):
        src = kv_ref.at[layer, :, :, pl.ds(g * GROUP_HEADS, GROUP_HEADS)]
        return pltpu.make_async_copy(src, kvb, kv_sem)

    kv_copy(0).start()

    barrier = pltpu.get_barrier_semaphore()
    for dev in (mate, xdev, ydev):
        pl.semaphore_signal(barrier, inc=1, device_id=dev, device_id_type=MESH)
    pl.semaphore_wait(barrier, 3)

    def send_own(g):
        for n in range(3):
            q_own(n, g).start()

    for g in range(Q_AHEAD):
        send_own(g)
    for g in range(groups):
        qall[0, g] = q_ref[g]

    def attend(g):
        kv_copy(g).wait()

        def order(rank, carry):
            request = at((rank // 2) % 2, rank % 2, rank // 4)
            for j in range(idx_ref.shape[1]):
                page = idx_ref[request, j]
                for side in range(2):
                    for h in range(GROUP_HEADS):
                        kvo[rank, side, h, j * page_len : (j + 1) * page_len, :] = kvb[page, side, h]
            return carry

        lax.fori_loop(0, 8, order, 0)

        @pl.when(g + 1 < groups)
        def _():
            kv_copy(g + 1).start()

        for s in range(4, 8):
            remote(qall.at[s, g], qall.at[s, g], qs_sem.at[0, g], qr_sem.at[s, g], mate).wait_recv()

        def half(turn, carry):
            other = 1 - turn
            for z in range(4):
                rank = other * 4 + z
                partial_attention(
                    part.at[rank, g], qall[rank, g], lambda h: kvo[rank, 0, h], lambda h: kvo[rank, 1, h], scale, dim
                )

            @pl.when(other == 1)
            def _():
                for n in range(4):
                    to_mate(n, g).start()

            return carry

        lax.fori_loop(0, 2, half, 0)
        cols = lambda h: slice(h * dim, (h + 1) * dim)
        key_row = lax.broadcasted_iota(jnp.int32, (tokens, tokens), 0)
        query_col = lax.broadcasted_iota(jnp.int32, (tokens, tokens), 1)
        partial_attention(
            part.at[8, g], q_ref[g], lambda h: kn_ref[g, :, cols(h)], lambda h: vn_ref[g, :, cols(h)],
            scale, dim, key_row <= query_col,
        )

    def finish(g):
        for n in range(2):
            home_send(n, g).wait_recv()
        blocks = [part.at[0, g], part.at[8, g], fin.at[0, g], fin.at[1, g]]
        base = GROUP_HEADS * dim
        stats = [b[base : base + 8, :] for b in blocks]
        for h in range(GROUP_HEADS):
            tops = [s[2 * h : 2 * h + 1] for s in stats]
            top = functools.reduce(jnp.maximum, tops)
            weights = [jnp.exp2(t - top) for t in tops]
            total = sum(w * s[2 * h + 1 : 2 * h + 2] for w, s in zip(weights, stats))
            mixed = sum(w * b[h * dim : (h + 1) * dim, :] for w, b in zip(weights, blocks)) / total
            cols = pl.ds(pl.multiple_of(g * base + h * dim, dim), dim)
            a_ref[:, cols] = jnp.transpose(mixed).astype(jnp.bfloat16)

    def stage(i, lag, fn):
        g = i - lag

        @pl.when(jnp.logical_and(g >= 0, g < groups))
        def _():
            fn(g)

    def both(g, fn):
        @pl.when(g % 2 == 0)
        def _():
            fn(True)

        @pl.when(g % 2 == 1)
        def _():
            fn(False)

    def relay_step(g):
        def run(via_x):
            diag_send(via_x, g).wait_recv()
            n = 1 if via_x else 0
            merge_into(part.at[1 + n, g], rel.at[g], dim)
            home_send(n, g).start()

        both(g, run)

    def merge_step(g):
        for n in (3, 1, 2, 0):
            to_mate(n, g).wait_recv()

        def run(via_x):
            merge_into(part.at[3, g], prx.at[3, g], dim)
            diag_send(via_x, g).start()
            first = 0 if via_x else 1
            merge_into(part.at[1 + first, g], prx.at[1 + first, g], dim)
            home_send(first, g).start()
            merge_into(part.at[2 - first, g], prx.at[2 - first, g], dim)

        both(g, run)
        merge_into(part.at[0, g], prx.at[0, g], dim)

    def q_first(g):
        @pl.when(g + Q_AHEAD < groups)
        def _():
            send_own(g + Q_AHEAD)

        for n in range(2):
            q_own(n, g).wait_recv()

        def run(via_x):
            q_relay(via_x, g).start()

        both(g, run)
        q_mate(1, g).start()
        q_mate(2, g).start()

    def q_second(g):
        q_relay(True, g).wait_recv()
        q_mate(3, g).start()

    def body(i, carry):
        stage(i, 4, relay_step)
        stage(i, 3, merge_step)
        stage(i, 0, q_first)
        stage(i, 1, q_second)
        stage(i, 2, attend)
        stage(i, 5, finish)
        return carry

    lax.fori_loop(0, groups + 5, body, 0)

    def drain(g, carry):
        for n in range(3):
            q_own(n, g).wait_send()
            q_mate(1 + n, g).wait_send()
        q_relay(True, g).wait_send()
        for n in range(4):
            to_mate(n, g).wait_send()
        diag_send(True, g).wait_send()
        for n in range(2):
            home_send(n, g).wait_send()
        return carry

    lax.fori_loop(0, groups, drain, 0)


def attention(layer, idx, query, key_new, val_new, kv):
    groups, tokens, cols = query.shape
    dim = cols // GROUP_HEADS
    pages, page_len = kv.shape[1], kv.shape[4]
    rows = cols + 8
    dma = pltpu.SemaphoreType.DMA
    vmem = pl.BlockSpec(memory_space=pltpu.VMEM)
    return pl.pallas_call(
        functools.partial(attn_kernel, layer, groups, dim),
        in_specs=[pl.BlockSpec(memory_space=pltpu.SMEM), vmem, vmem, vmem, pl.BlockSpec(memory_space=pl.ANY)],
        out_specs=vmem,
        out_shape=jax.ShapeDtypeStruct((tokens, groups * cols), jnp.bfloat16),
        scratch_shapes=[
            pltpu.VMEM((pages, 2, GROUP_HEADS, page_len, dim), jnp.bfloat16),
            pltpu.VMEM((8, 2, GROUP_HEADS, idx.shape[1] * page_len, dim), jnp.bfloat16),
            pltpu.VMEM((8, groups, tokens, cols), jnp.bfloat16),
            pltpu.VMEM((9, groups, rows, tokens), jnp.float32),
            pltpu.VMEM((4, groups, rows, tokens), jnp.float32),
            pltpu.VMEM((groups, rows, tokens), jnp.float32),
            pltpu.VMEM((2, groups, rows, tokens), jnp.float32),
            dma,
            dma((7, groups)),
            dma((8, groups)),
            dma((4, groups)),
            dma((4, groups)),
            dma((groups,)),
            dma((groups,)),
            dma((2, groups)),
            dma((2, groups)),
        ],
        compiler_params=pltpu.CompilerParams(collective_id=layer, has_side_effects=True, vmem_limit_bytes=60 << 20),
        name="attn",
    )(idx, query, key_new, val_new, kv)


def solution(mesh):
    group = mesh.shape["pool"]

    def local_program(kv_local, idx_local, hid_local, attn_norm, w_query, w_key, w_value, w_out, mlp_norm, w_gate, w_up, w_down):
        head_dim = kv_local.shape[-1]
        prefix = group * idx_local.shape[2] * kv_local.shape[3]
        cosine, sine = rope_tables(prefix, hid_local.shape[1], head_dim)
        kv = jnp.transpose(kv_local, (0, 1, 2, 4, 3, 5))
        idx = idx_local[:, 0, :]
        hidden = hid_local[0]
        for layer in range(kv_local.shape[0]):
            query, key_new, val_new = project_qkv(layer, hidden, attn_norm, cosine, sine, w_query, w_key, w_value, head_dim)
            attn = attention(layer, idx, query, key_new, val_new, kv)
            hidden = out_and_mlp(layer, hidden, attn, mlp_norm, w_out, w_gate, w_up, w_down)
        return hidden[None]

    data_specs = (P(None, ("rep", "pool")), P(None, ("rep", "pool"), None), P(("rep", "pool")))
    return jax.shard_map(local_program, mesh=mesh, in_specs=data_specs + (P(),) * 9, out_specs=P(("rep", "pool")), check_vma=False)
```

time: 1230 us -> 659 us (0.54)
  Pallas kernels: 0 us -> 655 us
  local copies, waits for them, and re-layouts: 407 us -> 1.35 us
  matrix products: 367 us -> 0 us
  waiting for transfers between devices: 335 us -> 0 us
  other arithmetic: 94.7 us -> 1.07 us
  starting transfers between devices: 20.3 us -> 0 us
    pallas_call x0 -> x12, Pallas kernels: none -> 655 us  [the longest x4 380 us: attention(): pl.pallas_call(functools.partial(attn_kernel, layer, groups, dim), in_spe...]
    dot_general x40 -> x0, matrix products: 367 us -> none  [the longest x4 109 us: decoder_layer(): jnp.dot(inner, down_weight, preferred_element_type=jnp.float32)]
    all_to_all x4 -> x0, waiting for transfers between devices: 335 us -> none  [local_program(): incoming = lax.all_to_all(outgoing, 'pool', 0, 0, tiled=True)]
    dot_general x10 -> x0, local copies, waits for them, and re-layouts: 212 us -> none  [the longest x5 106 us: decoder_layer(): jnp.dot(normed, q_weight, preferred_element_type=jnp.float32)]
    squeeze x1, local copies, waits for them, and re-layouts: 67.3 us -> 1.35 us  [local_program(): idx = idx_local[:, 0, :]]
    gather x4 -> x0, local copies, waits for them, and re-layouts: 62.8 us -> none  [local_program(): outgoing = jnp.take(kv_local[layer], page_rows, axis=0)]
    slice x4 -> x0, local copies, waits for them, and re-layouts: 59.8 us -> none  [attend(): val_pre = pages_kv[..., :, 1, :, :, :]]
    select_n x2 -> x0, other arithmetic: 53.1 us -> none  [local_program(): outgoing = jnp.take(kv_local[layer], page_rows, axis=0)]
  transfers between devices with their start and end apart: 4 -> 0, of which waited for: 3 -> 0; matrix products, arithmetic and copies ran while one was open for 48% -> 0% of each run, Pallas kernels for 0% -> 0%
where the time goes in v1:
time: 659 us; the launch traced here: 658 us
  Pallas kernels  655 us (99%)
    pallas_call x4, Pallas kernels, attention(): pl.pallas_call(functools.partial(attn_kernel, layer, groups, dim), in_spe...  380 us
    pallas_call x4, Pallas kernels, out_and_mlp(): pl.pallas_call(functools.partial(mlp_kernel, layer, o_steps, o_cols), gri...  201 us
    pallas_call x4, Pallas kernels, project_qkv(): pl.pallas_call(functools.partial(qkv_kernel, layer, head_dim), grid=(step...  74 us

profile of v1, /device:TPU:0, one launch (start us, length us, event | category | flops | bytes accessed | tf_op | source)
XLA Modules:
  0.0 657.6 jit_solution(359529913094902104)
XLA Ops:
  0.0 1.3 copy.13.idx_ref
  1.4 0.3 fusion
  1.7 0.8 pad_maximum_fusion
  2.4 18.5 %qkv.4 = (bf16[10,128,256]{2,1,0:T(8,128)(2,1)}, bf16[10,128,256]{2,1,0:T(8,128)(2,1)}, bf16[10,128,256]{2,1,0:T(8,128)(2,1)}) custom-call(bf16[128,2560]{1,0:T(8,128)(2,1)} %bitcast.4, bf16[4,2560]{1,0:T(4,128)(2,1)} %gain_ref.14, f32[128,128]{1,0:T(8,128)} %get-tuple-element.32.cos_ref, f32[128,128]{1,0:T(8,128)} %get-tuple-element.33.sin_ref, ...), custom_call_target="tpu_custom_call" | custom-call | tf_op jit(solution)/shard_map/qkv/pallas_call | solution.py:55
  20.9 97.2 %attn.4.a_ref = bf16[128,2560]{1,0:T(8,128)(2,1)} custom-call(s32[8,4]{1,0:T(8,128)} %copy.13.idx_ref, bf16[10,128,256]{2,1,0:T(8,128)(2,1)} %get-tuple-element.17.q_ref, bf16[10,128,256]{2,1,0:T(8,128)(2,1)} %get-tuple-element.18.kn_ref, bf16[10,128,256]{2,1,0:T(8,128)(2,1)} %get-tuple-element.19.vn_ref, bf16[4,32,2,20,64,128]{5,4,3,2,1,0:T(8,128)(2,1)} %bitcast.2.kv_ref), custom_call_target="tpu_custom_call" | custom-call | tf_op jit(solution)/shard_map/attn/pallas_call | solution.py:382
  118.2 50.2 %out_mlp.4.x_ref = bf16[128,2560]{1,0:T(8,128)(2,1)} custom-call(bf16[128,2560]{1,0:T(8,128)(2,1)} %bitcast.5, bf16[128,2560]{1,0:T(8,128)(2,1)} %attn.4.a_ref, bf16[4,2560]{1,0:T(4,128)(2,1)} %gain_ref.15, bf16[4,2560,2560]{2,1,0:T(8,128)(2,1)} %wo_ref.7, bf16[4,2560,6912]{2,1,0:T(8,128)(2,1)} %wg_ref.7, bf16[4,2560,6912]{2,1,0:T(8,128)(2,1)} %wu_ref.7, ...), custom_call_target="tpu_custom_call" | custom-call | tf_op jit(solution)/shard_map/out_mlp/pallas_call | solution.py:100
  168.4 18.5 %qkv.5 = (bf16[10,128,256]{2,1,0:T(8,128)(2,1)}, bf16[10,128,256]{2,1,0:T(8,128)(2,1)}, bf16[10,128,256]{2,1,0:T(8,128)(2,1)}) custom-call(bf16[128,2560]{1,0:T(8,128)(2,1)} %out_mlp.4.x_ref, bf16[4,2560]{1,0:T(4,128)(2,1)} %gain_ref.14, f32[128,128]{1,0:T(8,128)} %get-tuple-element.32.cos_ref, f32[128,128]{1,0:T(8,128)} %get-tuple-element.33.sin_ref, ...), custom_call_target="tpu_custom_call" | custom-call | tf_op jit(solution)/shard_map/qkv/pallas_call | solution.py:55
  186.9 94.1 %attn.5.a_ref = bf16[128,2560]{1,0:T(8,128)(2,1)} custom-call(s32[8,4]{1,0:T(8,128)} %copy.13.idx_ref, bf16[10,128,256]{2,1,0:T(8,128)(2,1)} %get-tuple-element.20.q_ref, bf16[10,128,256]{2,1,0:T(8,128)(2,1)} %get-tuple-element.21.kn_ref, bf16[10,128,256]{2,1,0:T(8,128)(2,1)} %get-tuple-element.22.vn_ref, bf16[4,32,2,20,64,128]{5,4,3,2,1,0:T(8,128)(2,1)} %bitcast.2.kv_ref), custom_call_target="tpu_custom_call" | custom-call | tf_op jit(solution)/shard_map/attn/pallas_call | solution.py:382
  281.0 50.2 %out_mlp.5.x_ref = bf16[128,2560]{1,0:T(8,128)(2,1)} custom-call(bf16[128,2560]{1,0:T(8,128)(2,1)} %out_mlp.4.x_ref, bf16[128,2560]{1,0:T(8,128)(2,1)} %attn.5.a_ref, bf16[4,2560]{1,0:T(4,128)(2,1)} %gain_ref.15, bf16[4,2560,2560]{2,1,0:T(8,128)(2,1)} %wo_ref.7, bf16[4,2560,6912]{2,1,0:T(8,128)(2,1)} %wg_ref.7, bf16[4,2560,6912]{2,1,0:T(8,128)(2,1)} %wu_ref.7, ...), custom_call_target="tpu_custom_call" | custom-call | tf_op jit(solution)/shard_map/out_mlp/pallas_call | solution.py:100
  331.1 18.5 %qkv.6 = (bf16[10,128,256]{2,1,0:T(8,128)(2,1)}, bf16[10,128,256]{2,1,0:T(8,128)(2,1)}, bf16[10,128,256]{2,1,0:T(8,128)(2,1)}) custom-call(bf16[128,2560]{1,0:T(8,128)(2,1)} %out_mlp.5.x_ref, bf16[4,2560]{1,0:T(4,128)(2,1)} %gain_ref.14, f32[128,128]{1,0:T(8,128)} %get-tuple-element.32.cos_ref, f32[128,128]{1,0:T(8,128)} %get-tuple-element.33.sin_ref, ...), custom_call_target="tpu_custom_call" | custom-call | tf_op jit(solution)/shard_map/qkv/pallas_call | solution.py:55
  349.6 95.0 %attn.6.a_ref = bf16[128,2560]{1,0:T(8,128)(2,1)} custom-call(s32[8,4]{1,0:T(8,128)} %copy.13.idx_ref, bf16[10,128,256]{2,1,0:T(8,128)(2,1)} %get-tuple-element.23.q_ref, bf16[10,128,256]{2,1,0:T(8,128)(2,1)} %get-tuple-element.24.kn_ref, bf16[10,128,256]{2,1,0:T(8,128)(2,1)} %get-tuple-element.25.vn_ref, bf16[4,32,2,20,64,128]{5,4,3,2,1,0:T(8,128)(2,1)} %bitcast.2.kv_ref), custom_call_target="tpu_custom_call" | custom-call | tf_op jit(solution)/shard_map/attn/pallas_call | solution.py:382
  444.7 50.2 %out_mlp.6.x_ref = bf16[128,2560]{1,0:T(8,128)(2,1)} custom-call(bf16[128,2560]{1,0:T(8,128)(2,1)} %out_mlp.5.x_ref, bf16[128,2560]{1,0:T(8,128)(2,1)} %attn.6.a_ref, bf16[4,2560]{1,0:T(4,128)(2,1)} %gain_ref.15, bf16[4,2560,2560]{2,1,0:T(8,128)(2,1)} %wo_ref.7, bf16[4,2560,6912]{2,1,0:T(8,128)(2,1)} %wg_ref.7, bf16[4,2560,6912]{2,1,0:T(8,128)(2,1)} %wu_ref.7, ...), custom_call_target="tpu_custom_call" | custom-call | tf_op jit(solution)/shard_map/out_mlp/pallas_call | solution.py:100
  494.9 18.5 %qkv.7 = (bf16[10,128,256]{2,1,0:T(8,128)(2,1)}, bf16[10,128,256]{2,1,0:T(8,128)(2,1)}, bf16[10,128,256]{2,1,0:T(8,128)(2,1)}) custom-call(bf16[128,2560]{1,0:T(8,128)(2,1)} %out_mlp.6.x_ref, bf16[4,2560]{1,0:T(4,128)(2,1)} %gain_ref.14, f32[128,128]{1,0:T(8,128)} %get-tuple-element.32.cos_ref, f32[128,128]{1,0:T(8,128)} %get-tuple-element.33.sin_ref, ...), custom_call_target="tpu_custom_call" | custom-call | tf_op jit(solution)/shard_map/qkv/pallas_call | solution.py:55
  513.4 94.1 %attn.7.a_ref = bf16[128,2560]{1,0:T(8,128)(2,1)} custom-call(s32[8,4]{1,0:T(8,128)} %copy.13.idx_ref, bf16[10,128,256]{2,1,0:T(8,128)(2,1)} %get-tuple-element.26.q_ref, bf16[10,128,256]{2,1,0:T(8,128)(2,1)} %get-tuple-element.27.kn_ref, bf16[10,128,256]{2,1,0:T(8,128)(2,1)} %get-tuple-element.28.vn_ref, bf16[4,32,2,20,64,128]{5,4,3,2,1,0:T(8,128)(2,1)} %bitcast.2.kv_ref), custom_call_target="tpu_custom_call" | custom-call | tf_op jit(solution)/shard_map/attn/pallas_call | solution.py:382
  607.5 50.2 %out_mlp.7 = bf16[128,2560]{1,0:T(8,128)(2,1)} custom-call(bf16[128,2560]{1,0:T(8,128)(2,1)} %out_mlp.6.x_ref, bf16[128,2560]{1,0:T(8,128)(2,1)} %attn.7.a_ref, bf16[4,2560]{1,0:T(4,128)(2,1)} %gain_ref.15, bf16[4,2560,2560]{2,1,0:T(8,128)(2,1)} %wo_ref.7, bf16[4,2560,6912]{2,1,0:T(8,128)(2,1)} %wg_ref.7, bf16[4,2560,6912]{2,1,0:T(8,128)(2,1)} %wu_ref.7, ...), custom_call_target="tpu_custom_call" | custom-call | tf_op jit(solution)/shard_map/out_mlp/pallas_call | solution.py:100
  (2 shorter events, 0.0 us)
